TPU v7x, 32 devices: a 4x4x1 block of a 4x4x8 slice. The times are simulated.
32 devices in a mesh: replica: 1 (over z), ep: 32 (over y, x, core).
Axes of the slice: x: 4, y: 4, z: 1, core: 2. Of those that a mesh axis runs over, the one named last changes fastest.
The devices are a block of a 4x4x8 slice.
Arguments:
- tok_in: bfloat16 [2048, 1536], P(('replica', 'ep'))
- routes: int32 [2, 2048, 6], P(None, ('replica', 'ep'))
- gate_vals: float32 [2, 2048, 6], P(None, ('replica', 'ep'))
- w_gate: bfloat16 [2, 64, 1536, 512], P(None, ('replica', 'ep'))
- w_up: bfloat16 [2, 64, 1536, 512], P(None, ('replica', 'ep'))
- w_down: bfloat16 [2, 64, 512, 1536], P(None, ('replica', 'ep'))
- sh_gate: bfloat16 [2, 1536, 1024], replicated
- sh_up: bfloat16 [2, 1536, 1024], replicated
- sh_down: bfloat16 [2, 1024, 1536], replicated
- old_map: int32 [2, 64], P(None, 'replica')
- move_slot: int32 [2, 2], P(None, 'replica')
- move_expert: int32 [2, 2], P(None, 'replica')
Outputs:
- output 1: bfloat16 [2048, 1536], P(('replica', 'ep'))
- output 2: bfloat16 [2, 64, 1536, 512], P(None, ('replica', 'ep'))
- output 3: bfloat16 [2, 64, 1536, 512], P(None, ('replica', 'ep'))
- output 4: bfloat16 [2, 64, 512, 1536], P(None, ('replica', 'ep'))
All inputs are finite; a program needn't handle non-finite values.
Results may differ from a plain program's by a relative error of at most 0.011583.
Values are sent between devices in bfloat16 or wider.
A program may use at most 768 MiB of HBM per device.

v0:
```python
import jax
import jax.numpy as jnp
from jax import lax
from jax.sharding import PartitionSpec as P

TOKEN_AXES = ('replica', 'ep')


def first_holder(slot_map, wanted):
    slot_ids = jnp.arange(slot_map.shape[0], dtype=jnp.int32)
    hit_mask = slot_map[None, :] == wanted[:, None]
    return jnp.min(jnp.where(hit_mask, slot_ids[None, :], slot_map.shape[0]), axis=1)


def swiglu(hidden, w_gate, w_up, w_down):
    gate_proj = jnp.dot(hidden, w_gate, preferred_element_type=jnp.float32)
    up_proj = jnp.dot(hidden, w_up, preferred_element_type=jnp.float32)
    inner_act = (jax.nn.silu(gate_proj) * up_proj).astype(jnp.bfloat16)
    return jnp.dot(inner_act, w_down, preferred_element_type=jnp.float32)


def send_moved(weights, slot_map, move_expert, slots_dev, my_dev):
    source = first_holder(slot_map, move_expert)
    is_source = (source // slots_dev) == my_dev
    local_idx = source % slots_dev
    return tuple(jnp.where(is_source[:, None, None], jnp.take(weight_arr, local_idx, axis=0), jnp.zeros((), weight_arr.dtype)) for weight_arr in weights)


def place_moved(weights, arrived, move_slot, slots_dev, my_dev):
    local_ids = my_dev * slots_dev + jnp.arange(slots_dev, dtype=jnp.int32)
    match_mask = (move_slot[None, :] == local_ids[:, None]).astype(jnp.int32)
    is_target = jnp.max(match_mask, axis=1) > 0
    pick_idx = jnp.argmax(match_mask, axis=1)
    return tuple(jnp.where(is_target[:, None, None], jnp.take(arrived_arr, pick_idx, axis=0), weight_arr) for arrived_arr, weight_arr in zip(arrived, weights))


def moe_layer(hidden, route_all, gate_all, expert_w, shared_w, slot_map, slots_dev, my_dev):
    gathered = lax.all_gather(hidden, 'ep', axis=0, tiled=True)
    slot_ids = jnp.arange(slot_map.shape[0], dtype=jnp.int32)
    serve_all = (first_holder(slot_map, slot_map) == slot_ids).astype(jnp.float32)
    local_map = lax.dynamic_slice_in_dim(slot_map, my_dev * slots_dev, slots_dev)
    local_serve = lax.dynamic_slice_in_dim(serve_all, my_dev * slots_dev, slots_dev)
    hit_mask = route_all[:, :, None] == local_map[None, None, :]
    gate_coef = jnp.sum(jnp.where(hit_mask, gate_all[:, :, None], 0.0), axis=1) * local_serve[None, :]
    gate_proj = jnp.einsum('nd,jdf->jnf', gathered, expert_w[0], preferred_element_type=jnp.float32)
    up_proj = jnp.einsum('nd,jdf->jnf', gathered, expert_w[1], preferred_element_type=jnp.float32)
    inner_act = (jax.nn.silu(gate_proj) * up_proj).astype(jnp.bfloat16)
    expert_out = jnp.einsum('jnf,jfd->jnd', inner_act, expert_w[2], preferred_element_type=jnp.float32)
    partial_sum = jnp.sum(expert_out * gate_coef.T[:, :, None], axis=0)
    combined = lax.psum_scatter(partial_sum, 'ep', scatter_dimension=0, tiled=True)
    shared_out = swiglu(hidden, shared_w[0], shared_w[1], shared_w[2])
    return (hidden.astype(jnp.float32) + shared_out + combined).astype(jnp.bfloat16)


def solution(mesh):
    def body(tok_in, routes, gate_vals, w_gate, w_up, w_down, sh_gate, sh_up, sh_down, old_map, move_slot, move_expert):
        my_dev = lax.axis_index('ep')
        slots_dev = w_gate.shape[1]
        route_all = lax.all_gather(routes, 'ep', axis=1, tiled=True)
        gate_all = lax.all_gather(gate_vals, 'ep', axis=1, tiled=True)
        hidden = tok_in
        placed = []
        for layer_idx in range(2):
            layer_w = (w_gate[layer_idx], w_up[layer_idx], w_down[layer_idx])
            outgoing = send_moved(layer_w, old_map[layer_idx], move_expert[layer_idx], slots_dev, my_dev)
            arrived = lax.psum(outgoing, 'ep')
            new_w = place_moved(layer_w, arrived, move_slot[layer_idx], slots_dev, my_dev)
            new_map = old_map[layer_idx].at[move_slot[layer_idx]].set(move_expert[layer_idx])
            shared_w = (sh_gate[layer_idx], sh_up[layer_idx], sh_down[layer_idx])
            hidden = moe_layer(hidden, route_all[layer_idx], gate_all[layer_idx], new_w, shared_w, new_map, slots_dev, my_dev)
            placed.append(new_w)
        new_gate = jnp.stack([placed[0][0], placed[1][0]])
        new_up = jnp.stack([placed[0][1], placed[1][1]])
        new_down = jnp.stack([placed[0][2], placed[1][2]])
        return (hidden, new_gate, new_up, new_down)

    weight_spec = P(None, TOKEN_AXES, None, None)
    route_spec = P(None, TOKEN_AXES, None)
    map_spec = P(None, 'replica')
    shared_spec = P(None, None, None)
    tok_spec = P(TOKEN_AXES, None)
    return jax.shard_map(body, mesh=mesh, in_specs=(tok_spec, route_spec, route_spec, weight_spec, weight_spec, weight_spec, shared_spec, shared_spec, shared_spec, map_spec, map_spec, map_spec), out_specs=(tok_spec, weight_spec, weight_spec, weight_spec), check_vma=False)
```

profile of v0, /device:TPU:98, one launch (start us, length us, event | category | flops | bytes accessed | tf_op | source)
XLA Modules:
  0.0 622.2 jit_solution(16419846987130318962)
XLA Ops:
  7.2 0.8 slice_bitcast_fusion.9
  8.0 0.8 slice_bitcast_fusion.8
  8.8 4.9 slice_bitcast_fusion.2
  13.7 0.2 fusion.98
  13.9 6.0 slice_bitcast_fusion.1
  19.9 4.3 gather_fusion
  24.2 4.3 gather_fusion.2
  28.5 5.9 slice_bitcast_fusion
  34.4 4.3 gather_fusion.4
  38.8 2.5 gather_fusion.6
  41.2 2.6 gather_fusion.8
  43.9 4.3 gather_fusion.10
  48.1 4.1 select_select_fusion.7
  52.2 0.5 copy-done.2
  52.7 3.4 select_select_fusion.11
  56.2 2.1 select_select_fusion.1
  58.3 0.9 copy-done.3
  59.2 3.4 select_select_fusion.5
  62.7 0.7 all-gather.3.cloned.1.call-update
  63.5 0.1 copy.55
  63.7 0.1 copy.53
  63.8 40.5 %all_gather.14 = f32[2,2048,6]{2,0,1:T(2,128)S(1)} all-gather(f32[2,64,6]{2,0,1:T(2,128)S(1)} %copy.55), channel_id=1, replica_groups=mesh['replica'=1,'ep'=32] {'ep'}, dimensions={1}, use_global_device_ids=true | all-gather | bytes 101376 | tf_op jit(solution)/shard_map/all_gather | solution.py:60
  104.3 2.5 fusion.115
  106.8 0.5 copy.69
  107.3 49.7 %all_gather.13 = s32[2,2048,6]{2,0,1:T(2,128)S(1)} all-gather(s32[2,64,6]{2,0,1:T(2,128)S(1)} %copy.53), channel_id=1, replica_groups=mesh['replica'=1,'ep'=32] {'ep'}, dimensions={1}, use_global_device_ids=true | all-gather | bytes 101376 | tf_op jit(solution)/shard_map/all_gather | solution.py:59
  157.0 2.5 fusion.114
  159.5 0.5 copy.68
  160.1 0.6 scatter_fusion
  160.7 0.2 select_reduce_fusion.1
  161.0 0.7 fusion.94
  161.7 0.2 fusion.97
  161.9 0.1 fusion.92
  162.1 84.7 %all-reduce.3.cloned.1.call-done = (bf16[2,1536,512]{2,1,0:T(8,128)(2,1)}, bf16[2,1536,512]{2,1,0:T(8,128)(2,1)}, bf16[2,512,1536]{2,1,0:T(8,128)(2,1)}, bf16[2,...) async-done(((bf16[2,1536,512]{2,1,0:T(8,128)(2,1)}, bf16[2,1536,512]{2,1,0:T(8,128)(2,1)}, bf16[2,512,1536]{2,1,0:T(8,128)(2,1)}, ...) | async-done | bytes 18874384 | tf_op jit(solution)/shard_map/psum | solution.py:66
  246.8 4.4 gather_fusion.3
  251.3 2.4 gather_fusion.1
  253.7 2.6 gather_fusion.5
  256.3 36.4 %all-gather.3.cloned.1.call-done = bf16[2048,1536]{1,0:T(8,128)(2,1)} async-done(((bf16[64,1536]{1,0:T(8,128)(2,1)}), bf16[2048,1536]{1,0:T(8,128)(2,1)}) %all-gather.3.cloned.1.call-update) | async-done | bytes 6291472 | tf_op jit(solution)/shard_map/all_gather | solution.py:38
  292.7 12.9 %fusion.12 = f32[2,512,2048]{2,1,0:T(8,128)} fusion(bf16[2048,1536]{1,0:T(8,128)(2,1)} %all-gather.3.cloned.1.call-done, bf16[2,1536,512]{2,1,0:T(8,128)(2,1)} %gather_fusion.3, pred[2]{0:T(512)(128)(4,1)S(1)} %get-tuple-element.56, pred[2]{0:T(512)(128)(4,1)S(1)} %get-tuple-element.57, bf16[2,2,1536,512]{3,2,1,0:T(8,128)(2,1)} %param.20), kind=kOutput, calls=%fused_computation.37 | convolution fusion | flops 6445596672 | bytes 20971524 | tf_op jit(solution)/shard_map/nd,jdf->jnf/dot_general | solution.py:46
  305.5 25.7 %multiply_reduce_fusion.1 = f32[2048,1536]{1,0:T(8,128)} fusion(f32[2,2048]{1,0:T(2,128)S(1)} %multiply_bitcast_fusion.1, f32[2,512,2048]{2,1,0:T(8,128)} %fusion.12, bf16[2048,1536]{1,0:T(8,128)(2,1)} %all-gather.3.cloned.1.call-done, bf16[2,1536,512]{2,1,0:T(8,128)(2,1)} %gather_fusion.1, pred[2]{0:T(512)(128)(4,1)S(1)} %get-tuple-element.56, ...), kind=kOutput, calls=%fused_computation.15 | convolution fusion | flops 12913213440 | bytes 39864320 | tf_op jit(solution)/shard_map/jnf,jfd->jnd/dot_general | solution.py:48
  331.3 0.8 copy-done.6
  332.1 3.3 fusion.30
  335.4 92.3 %reduce-scatter.3.cloned.1.call-done = f32[64,1536]{1,0:T(8,128)} async-done(((f32[2048,1536]{1,0:T(8,128)}), f32[64,1536]{1,0:T(8,128)}) %reduce-scatter.3.cloned.1.call-update) | async-done | bytes 393232 | tf_op jit(solution)/shard_map/reduce_scatter | solution.py:50
  427.7 4.9 fusion.61
  432.7 2.3 copy.71
  434.9 2.3 copy.70
  437.2 0.8 scatter_fusion.1
  438.1 0.2 select_reduce_fusion
  438.4 0.7 fusion.96
  439.1 0.1 fusion.93
  439.3 4.3 gather_fusion.9
  443.6 4.3 gather_fusion.7
  447.8 4.3 gather_fusion.11
  452.1 22.8 %all-gather.5.cloned.1.call-done = bf16[2048,1536]{1,0:T(8,128)(2,1)} async-done(((bf16[64,1536]{1,0:T(8,128)(2,1)}), bf16[2048,1536]{1,0:T(8,128)(2,1)}) %all-gather.5.cloned.1.call-update) | async-done | bytes 6291472 | tf_op jit(solution)/shard_map/all_gather | solution.py:38
  474.9 12.9 %fusion.8 = f32[2,512,2048]{2,1,0:T(8,128)} fusion(bf16[2048,1536]{1,0:T(8,128)(2,1)} %all-gather.5.cloned.1.call-done, bf16[2,1536,512]{2,1,0:T(8,128)(2,1)} %gather_fusion.9, pred[2]{0:T(512)(128)(4,1)S(1)} %get-tuple-element.58, pred[2]{0:T(512)(128)(4,1)S(1)} %get-tuple-element.59, bf16[2,2,1536,512]{3,2,1,0:T(8,128)(2,1)} %param.20), kind=kOutput, calls=%fused_computation.33 | convolution fusion | flops 6445596672 | bytes 20971524 | tf_op jit(solution)/shard_map/nd,jdf->jnf/dot_general | solution.py:46
  487.8 26.2 %multiply_reduce_fusion = f32[2048,1536]{1,0:T(8,128)} fusion(f32[2,2048]{1,0:T(2,128)S(1)} %multiply_bitcast_fusion, f32[2,512,2048]{2,1,0:T(8,128)} %fusion.8, bf16[2048,1536]{1,0:T(8,128)(2,1)} %all-gather.5.cloned.1.call-done, bf16[2,1536,512]{2,1,0:T(8,128)(2,1)} %gather_fusion.7, pred[2]{0:T(512)(128)(4,1)S(1)} %get-tuple-element.58, ...), kind=kOutput, calls=%fused_computation.14 | convolution fusion | flops 12913213440 | bytes 39864320 | tf_op jit(solution)/shard_map/jnf,jfd->jnd/dot_general | solution.py:48
  514.1 10.7 %fusion.108 = (bf16[1,2,1536,512]{3,2,1,0:T(8,128)(2,1)S(1)}, bf16[1,2,1536,512]{3,2,1,0:T(8,128)(2,1)}, bf16[1,2,1536,512]{3,2,1,0:T(8,128)(2,1)S(1)}, bf16[1,2,1536,512]{3,2,1,0:T(8,128)(2,1)S(1)}) fusion(bf16[2,2,1536,512]{3,2,1,0:T(8,128)(2,1)} %param.19, bf16[2,1536,512]{2,1,0:T(8,128)(2,1)} %gather_fusion.1, pred[2]{0:T(512)(128)(4,1)S(1)} %get-tuple-element.56, ...), kind=kLoop, calls=%fused_computation.162 | loop fusion | flops 12582912 | bytes 37748744 | tf_op jit(solution)/shard_map/stack | solution.py:72
  524.8 5.3 pad_maximum_fusion
  530.1 3.7 pad_maximum_fusion.1
  533.8 1.0 copy-done
  534.9 1.1 fusion.110
  536.0 3.2 pad_maximum_fusion.2
  539.2 2.6 fusion.24
  541.8 68.6 %reduce-scatter.5.cloned.1.call-done = f32[64,1536]{1,0:T(8,128)} async-done(((f32[2048,1536]{1,0:T(8,128)}), f32[64,1536]{1,0:T(8,128)}) %reduce-scatter.5.cloned.1.call-update) | async-done | bytes 393232 | tf_op jit(solution)/shard_map/reduce_scatter | solution.py:50
  610.5 4.8 fusion.58
  (53 shorter events, 1.1 us)
Async XLA Ops:
  7.2 239.6 %all-reduce.3.cloned.1.call-start = ((), (), s32[]{:S(2)}) async-start(), calls=%async_computation.6 | async-start | bytes 37748736 | tf_op jit(solution)/shard_map/psum | solution.py:66
  48.1 4.1 copy-start.1
  48.1 4.6 copy-start.2
  52.7 3.4 copy-start.4
  56.2 3.0 copy-start.3
  62.6 1.0 copy-start.8
  62.6 1.1 copy-start.9
  62.6 230.0 %all-gather.3.cloned.1.call-start = ((), (), s32[]{:S(2)}) async-start(), calls=%async_computation.2 | async-start | bytes 6488064 | tf_op jit(solution)/shard_map/all_gather | solution.py:38
  63.5 364.2 %reduce-scatter.3.cloned.1.call-start = ((), (), s32[]{:S(2)}) async-start(), calls=%async_computation.3 | async-start | bytes 12976128 | tf_op jit(solution)/shard_map/reduce_scatter | solution.py:50
  157.0 3.0 copy-start.10
  246.8 4.5 copy-start.5
  331.2 0.9 copy-start.6
  331.3 143.7 %all-gather.5.cloned.1.call-start = ((), (), s32[]{:S(2)}) async-start(), calls=%async_computation.4 | async-start | bytes 6488064 | tf_op jit(solution)/shard_map/all_gather | solution.py:38
  432.6 177.9 %reduce-scatter.5.cloned.1.call-start = ((), (), s32[]{:S(2)}) async-start(), calls=%async_computation.5 | async-start | bytes 12976128 | tf_op jit(solution)/shard_map/reduce_scatter | solution.py:50
  524.8 9.1 %slice-start = ((s8[6291456]{0:T(1024)(128)(4,1)}), s8[4194304]{0:T(1024)(128)(4,1)S(1)}, s32[]{:S(2)}) async-start(s8[6291456]{0:T(1024)(128)(4,1)} %bitcast.186), calls=%async_computation.7 | async-start | bytes 8388608
  530.1 3.7 slice-start.1
  530.1 4.8 copy-start
  536.0 3.3 copy-start.7
Sparse Core Ops, SparseCore 0:
  62.8 183.9 all-reduce.2
  248.9 43.7 all-gather.2
  331.4 96.2 reduce-scatter.2
  432.7 42.1 all-gather.4
  514.2 96.2 reduce-scatter.4
where the time goes:
time: 630 us; the launch traced here: 622 us
  waiting for transfers between devices  306 us (49%)
  matrix products  93.1 us (15%)
  blocking collectives  90.2 us (14%)
  local copies, waits for them, and re-layouts  78.7 us (12%)
  other arithmetic  39.7 us (6%)
  between operations  14.4 us (2%)
    reduce_scatter x2, waiting for transfers between devices, moe_layer(): lax.psum_scatter(partial_sum, 'ep', scatter_dimension=0, tiled=True)  161 us
    psum x1, waiting for transfers between devices, body(): arrived = lax.psum(outgoing, 'ep')  84.7 us
    all_gather x2, waiting for transfers between devices, moe_layer(): gathered = lax.all_gather(hidden, 'ep', axis=0, tiled=True)  59.2 us
    dot_general x2, matrix products, moe_layer(): jnp.einsum('jnf,jfd->jnd', inner_act, expert_w[2], preferred_element_type...  51.9 us
    all_gather x1, blocking collectives, body(): route_all = lax.all_gather(routes, 'ep', axis=1, tiled=True)  49.7 us
    all_gather x1, blocking collectives, body(): gate_all = lax.all_gather(gate_vals, 'ep', axis=1, tiled=True)  40.5 us
    dot_general x2, matrix products, moe_layer(): jnp.einsum('nd,jdf->jnf', gathered, expert_w[1], preferred_element_type=j...  25.7 us
    gather x6, local copies, waits for them, and re-layouts, place_moved(): jnp.take(arrived_arr, pick_idx, axis=0)  22.3 us
  transfers between devices with their start and end apart: 5, of which 5 were waited for; matrix products, arithmetic and copies ran while one was open for 11% of the time, Pallas kernels for 0%

commit v1 on v0

v1 whole, which is shorter than its diff:
```python
import functools

import jax
import jax.numpy as jnp
from jax import lax
from jax.experimental import pallas as pl
from jax.experimental.pallas import tpu as pltpu
from jax.sharding import PartitionSpec as P

TOKEN_AXES = ('replica', 'ep')
MESH = pl.DeviceIdType.MESH
F32 = jnp.float32
BF16 = jnp.bfloat16


def first_holder(slot_map, wanted):
    slot_ids = jnp.arange(slot_map.shape[0], dtype=jnp.int32)
    hit_mask = slot_map[None, :] == wanted[:, None]
    return jnp.min(jnp.where(hit_mask, slot_ids[None, :], slot_map.shape[0]), axis=1)


def send_moved(weights, slot_map, move_expert, slots_dev, my_dev):
    source = first_holder(slot_map, move_expert)
    is_source = (source // slots_dev) == my_dev
    local_idx = source % slots_dev
    return tuple(jnp.where(is_source[:, None, None], jnp.take(weight_arr, local_idx, axis=0), jnp.zeros((), weight_arr.dtype)) for weight_arr in weights)


def place_moved(weights, arrived, move_slot, slots_dev, my_dev):
    local_ids = my_dev * slots_dev + jnp.arange(slots_dev, dtype=jnp.int32)
    match_mask = (move_slot[None, :] == local_ids[:, None]).astype(jnp.int32)
    is_target = jnp.max(match_mask, axis=1) > 0
    pick_idx = jnp.argmax(match_mask, axis=1)
    return tuple(jnp.where(is_target[:, None, None], jnp.take(arrived_arr, pick_idx, axis=0), weight_arr) for arrived_arr, weight_arr in zip(arrived, weights))


def gate_table(routes, gate_vals, old_map):
    cols = []
    slot_ids = jnp.arange(old_map.shape[1], dtype=jnp.int32)
    for layer in range(old_map.shape[0]):
        serve = first_holder(old_map[layer], old_map[layer]) == slot_ids
        hit = (routes[layer][:, :, None] == old_map[layer][None, None, :]) & serve[None, None, :]
        cols.append(jnp.sum(jnp.where(hit, gate_vals[layer][:, :, None], 0.0), axis=1))
    return jnp.concatenate(cols, axis=1)


def moe_kernel(side, tok, coef, wg, wu, wd, sg, su, sd, out,
               xb, cb, wgv, wuv, wdv, sgv, suv, sdv, act, hacc, own, pcs, pcr, rs,
               wsem, ssem, tsem, xsend, xrecv, msend, mrecv, csend, crecv, cmsend, cmrecv,
               psend, precv, rsend, rrecv, mid):
    layers, slots, dim, ff = wg.shape
    rows = tok.shape[0]
    half = rows // 2
    n = side * side
    me = lax.axis_index('ep')
    core = lax.rem(me, 2)
    chip = lax.div(me, 2)
    yy = lax.div(chip, side)
    xx = lax.rem(chip, side)
    ga = yy * (1 - core) + xx * core
    gb = xx * (1 - core) + yy * core
    pos = side * ga + lax.rem(ga + gb, side)

    def ring_dev(k):
        k = lax.rem(k, n)
        a = lax.div(k, side)
        b = lax.rem(lax.rem(k, side) - a + side, side)
        y = a * (1 - core) + b * core
        x = b * (1 - core) + a * core
        return (y * side + x) * 2 + core

    peers = (ring_dev(pos + 1), ring_dev(pos + n - 1))
    mate = me + 1 - 2 * core

    def remote(src, dst, ss, rr, dev):
        return pltpu.make_async_remote_copy(src_ref=src, dst_ref=dst, send_sem=ss, recv_sem=rr,
                                            device_id={'ep': dev}, device_id_type=MESH)

    def part(d):
        return pl.ds(d * half, half)

    mine, theirs = pl.ds(0, rows), pl.ds(rows, rows)

    def xcopy(l, s, d):
        return remote(xb.at[l, s, part(d)], xb.at[l, s + 1, part(d)], xsend.at[l, s, d], xrecv.at[l, s + 1, d], peers[d])

    def mcopy(l, s):
        return remote(xb.at[l, s, mine], xb.at[l, s, theirs], msend.at[l, s], mrecv.at[l, s], mate)

    def ccopy(s, d):
        return remote(cb.at[s, part(d)], cb.at[s + 1, part(d)], csend.at[s, d], crecv.at[s + 1, d], peers[d])

    def cmcopy(s):
        return remote(cb.at[s, mine], cb.at[s, theirs], cmsend.at[s], cmrecv.at[s], mate)

    def pcopy(l, s):
        return remote(pcs.at[lax.rem(s, 2)], pcr.at[s], psend.at[lax.rem(s, 2)], precv.at[l, s], mate)

    def rcopy(l, s, d):
        return remote(rs.at[s, part(d)], rs.at[s + 1, part(d)], rsend.at[l, s, d], rrecv.at[l, s + 1, d], peers[d])

    def shared_loads(l):
        return [pltpu.make_async_copy(src.at[l], dst, ssem.at[l, i]) for i, (src, dst) in enumerate(((sg, sgv), (su, suv), (sd, sdv)))]

    def expert_loads(l):
        return [pltpu.make_async_copy(src.at[l], dst.at[l], wsem.at[l, i]) for i, (src, dst) in enumerate(((wg, wgv), (wu, wuv), (wd, wdv)))]

    tok_in = pltpu.make_async_copy(tok, xb.at[0, 0, mine], tsem.at[0])
    coef_in = pltpu.make_async_copy(coef, cb.at[0, mine], tsem.at[1])
    tok_in.start()
    coef_in.start()
    for copy in shared_loads(0):
        copy.start()
    for l in range(layers):
        for copy in expert_loads(l):
            copy.start()

    barrier = pltpu.get_barrier_semaphore()
    for dev in peers + (mate,):
        pl.semaphore_signal(barrier, inc=1, device_id={'ep': dev}, device_id_type=MESH)
    pl.semaphore_wait(barrier, 3)
    tok_in.wait()
    coef_in.wait()

    def forward(l, s):
        for d in range(2):
            xcopy(l, s, d).start()
            if l == 0:
                ccopy(s, d).start()

    def to_mate(l, s):
        mcopy(l, s).start()
        if l == 0:
            cmcopy(s).start()

    def wait_block(l, s):
        for d in range(2):
            xcopy(l, s - 1, d).wait_recv()
            if l == 0:
                ccopy(s - 1, d).wait_recv()

    def wait_mate(l, s):
        mcopy(l, s).wait_recv()
        if l == 0:
            cmcopy(s).wait_recv()

    fblk = min(ff, 256)
    dblk = min(dim, 512)

    def experts(l, s):
        x = xb.at[l, s]
        table = cb[s]
        lane = lax.broadcasted_iota(jnp.int32, table.shape, 1)
        weight = []
        for i in range(slots):
            col = l * (coef.shape[1] // layers) + me * slots + i
            weight.append(jnp.sum(jnp.where(lane == col, table, 0.0), axis=1, keepdims=True))
            for f in range(0, ff, fblk):
                g = jnp.dot(x[...], wgv[l, i, :, f:f + fblk], preferred_element_type=F32)
                u = jnp.dot(x[...], wuv[l, i, :, f:f + fblk], preferred_element_type=F32)
                act[i, :, f:f + fblk] = (jax.nn.silu(g) * u).astype(BF16)
        slot = lax.rem(s, 2)
        for c in range(0, dim, dblk):
            total = None
            for i in range(slots):
                o = jnp.dot(act[i], wdv[l, i, :, c:c + dblk], preferred_element_type=F32) * weight[i]
                total = o if total is None else total + o
            own[:, c:c + dblk] = total[:rows]
            pcs[slot, :, c:c + dblk] = total[rows:]

    for l in range(layers):
        forward(l, 0)
        to_mate(l, 0)
        if l > 0:
            drain(l - 1)
            for dev in peers + (mate,):
                pl.semaphore_signal(mid, inc=1, device_id={'ep': dev}, device_id_type=MESH)
        for copy in shared_loads(l):
            copy.wait()
        h = xb.at[l, 0, mine]
        sff = sgv.shape[1]
        for f in range(0, sff, fblk):
            g = jnp.dot(h[...], sgv[:, f:f + fblk], preferred_element_type=F32)
            u = jnp.dot(h[...], suv[:, f:f + fblk], preferred_element_type=F32)
            act_sh = (jax.nn.silu(g) * u).astype(BF16)
            act[f // ff, 0:rows, f % ff:f % ff + fblk] = act_sh
        for c in range(0, dim, dblk):
            total = h[:, c:c + dblk].astype(F32)
            for f in range(0, sff, ff):
                w = min(ff, sff - f)
                total = total + jnp.dot(act[f // ff, 0:rows, 0:w], sdv[f:f + w, c:c + dblk], preferred_element_type=F32)
            hacc[:, c:c + dblk] = total
        if l + 1 < layers:
            for copy in shared_loads(l + 1):
                copy.start()
        for copy in expert_loads(l):
            copy.wait()
        if l > 0:
            pl.semaphore_wait(mid, 3)
        wait_mate(l, 0)
        experts(l, 0)
        pcopy(l, 0).start()
        hacc[...] += own[...]
        wait_block(l, 1)
        forward(l, 1)
        to_mate(l, 1)

        def step(s, carry):
            wait_mate(l, s)

            @pl.when(s >= 2)
            def _():
                pcopy(l, s - 2).wait_send()

            experts(l, s)
            pcopy(l, s).start()

            @pl.when(s < n - 1)
            def _():
                wait_block(l, s + 1)
                to_mate(l, s + 1)

            @pl.when(s < n - 2)
            def _():
                forward(l, s + 1)

            pcopy(l, s).wait_recv()

            @pl.when(s == 1)
            def _():
                rs[s] = own[...] + pcr[s]

            @pl.when(s > 1)
            def _():
                for d in range(2):
                    rcopy(l, s - 1, d).wait_recv()
                rs[s] = rs[s] + (own[...] + pcr[s])

            for d in range(2):
                rcopy(l, s, d).start()
            return carry

        lax.fori_loop(1, n, step, 0)
        for d in range(2):
            rcopy(l, n - 1, d).wait_recv()
        pcopy(l, 0).wait_recv()
        new_h = (hacc[...] + (pcr[0] + rs[n])).astype(BF16)
        if l + 1 < layers:
            xb[l + 1, 0, mine] = new_h
        else:
            out[...] = new_h

        def drain(l):
            pcopy(l, n - 2).wait_send()
            pcopy(l, n - 1).wait_send()
            mcopy(l, 0).wait_send()
            if l == 0:
                cmcopy(0).wait_send()
            for d in range(2):
                xcopy(l, 0, d).wait_send()
                if l == 0:
                    ccopy(0, d).wait_send()

            def one(s, carry):
                mcopy(l, s).wait_send()
                if l == 0:
                    cmcopy(s).wait_send()
                for d in range(2):
                    rcopy(l, s, d).wait_send()

                @pl.when(s < n - 1)
                def _():
                    for d in range(2):
                        xcopy(l, s, d).wait_send()
                        if l == 0:
                            ccopy(s, d).wait_send()
                return carry

            lax.fori_loop(1, n, one, 0)

    drain(layers - 1)


def moe(tok, coef, wg, wu, wd, sg, su, sd, group):
    layers, slots, dim, ff = wg.shape
    rows = tok.shape[0]
    sff = sg.shape[2]
    n = group // 2
    side = int(round(n ** 0.5))
    assert side * side * 2 == group
    dma = pltpu.SemaphoreType.DMA
    any_spec = pl.BlockSpec(memory_space=pl.ANY)
    vmem = pltpu.VMEM
    act_n = max(slots, -(-sff // ff))
    scratch = [
        vmem((layers, n, 2 * rows, dim), BF16),
        vmem((n, 2 * rows, coef.shape[1]), F32),
        vmem((layers, slots, dim, ff), BF16),
        vmem((layers, slots, dim, ff), BF16),
        vmem((layers, slots, ff, dim), BF16),
        vmem((dim, sff), BF16),
        vmem((dim, sff), BF16),
        vmem((sff, dim), BF16),
        vmem((act_n, 2 * rows, ff), BF16),
        vmem((rows, dim), F32),
        vmem((rows, dim), F32),
        vmem((2, rows, dim), F32),
        vmem((n, rows, dim), F32),
        vmem((n + 1, rows, dim), F32),
        dma((layers, 3)), dma((layers, 3)), dma((2,)),
        dma((layers, n, 2)), dma((layers, n, 2)),
        dma((layers, n)), dma((layers, n)),
        dma((n, 2)), dma((n, 2)),
        dma((n,)), dma((n,)),
        dma((2,)), dma((layers, n)),
        dma((layers, n, 2)), dma((layers, n + 1, 2)),
        pltpu.SemaphoreType.REGULAR,
    ]
    flops = layers * 2 * 3 * dim * (ff * slots * rows * group + sff * rows)
    return pl.pallas_call(
        functools.partial(moe_kernel, side),
        out_shape=jax.ShapeDtypeStruct((rows, dim), BF16),
        in_specs=[any_spec] * 8,
        out_specs=pl.BlockSpec(memory_space=pltpu.VMEM),
        scratch_shapes=scratch,
        compiler_params=pltpu.CompilerParams(collective_id=0, has_side_effects=True, vmem_limit_bytes=67043328),
        cost_estimate=pl.CostEstimate(flops=flops * 4, bytes_accessed=40 << 20, transcendentals=0),
        name='moe_rings',
    )(tok, coef, wg, wu, wd, sg, su, sd)


def solution(mesh):
    group = mesh.shape['ep']

    def body(tok_in, routes, gate_vals, w_gate, w_up, w_down, sh_gate, sh_up, sh_down, old_map, move_slot, move_expert):
        my_dev = lax.axis_index('ep')
        layers, slots_dev = w_gate.shape[:2]
        placed = []
        for layer in range(layers):
            layer_w = (w_gate[layer], w_up[layer], w_down[layer])
            outgoing = send_moved(layer_w, old_map[layer], move_expert[layer], slots_dev, my_dev)
            arrived = lax.psum(outgoing, 'ep')
            placed.append(place_moved(layer_w, arrived, move_slot[layer], slots_dev, my_dev))
        coef = gate_table(routes, gate_vals, old_map)
        hidden = moe(tok_in, coef, w_gate, w_up, w_down, sh_gate, sh_up, sh_down, group)
        new_w = tuple(jnp.stack([p[i] for p in placed]) for i in range(3))
        return (hidden,) + new_w

    weight_spec = P(None, TOKEN_AXES, None, None)
    route_spec = P(None, TOKEN_AXES, None)
    map_spec = P(None, 'replica')
    shared_spec = P(None, None, None)
    tok_spec = P(TOKEN_AXES, None)
    return jax.shard_map(body, mesh=mesh, in_specs=(tok_spec, route_spec, route_spec, weight_spec, weight_spec, weight_spec, shared_spec, shared_spec, shared_spec, map_spec, map_spec, map_spec), out_specs=(tok_spec, weight_spec, weight_spec, weight_spec), check_vma=False)
```

time: 630 us -> 380 us (0.60); the launches traced: 622 us -> 378 us
  waiting for transfers between devices: 306 us -> 0.07 us
  Pallas kernels: 0 us -> 250 us
  matrix products: 93.1 us -> 0 us
  blocking collectives: 90.2 us -> 0 us
  local copies, waits for them, and re-layouts: 78.7 us -> 67.3 us
  other arithmetic: 39.7 us -> 47.2 us
    pallas_call x0 -> x1, Pallas kernels: none -> 250 us  [moe(): pl.pallas_call(functools.partial(moe_kernel, side), out_shape=jax.ShapeDt...]
    reduce_scatter x2 -> x0, waiting for transfers between devices: 161 us -> none  [moe_layer(): lax.psum_scatter(partial_sum, 'ep', scatter_dimension=0, tiled=True)]
    dot_general x8 -> x0, matrix products: 93.1 us -> none  [the longest x2 51.9 us: moe_layer(): jnp.einsum('jnf,jfd->jnd', inner_act, expert_w[2], preferred_element_type...]
    all_gather x2 -> x0, blocking collectives: 90.2 us -> none  [the longest x1 49.7 us: body(): route_all = lax.all_gather(routes, 'ep', axis=1, tiled=True)]
    psum x1, waiting for transfers between devices: 84.7 us -> 0.02 us  [body(): arrived = lax.psum(outgoing, 'ep')]
    all_gather x2 -> x0, waiting for transfers between devices: 59.2 us -> none  [moe_layer(): gathered = lax.all_gather(hidden, 'ep', axis=0, tiled=True)]
    another operation x5, other arithmetic: 24.1 us -> 31 us  [body(): new_w = tuple((jnp.stack([p[i] for p in placed]) for i in range(3)))]
  transfers between devices with their start and end apart: 5 -> 1, of which waited for: 5 -> 0; matrix products, arithmetic and copies ran while one was open for 11% -> 1% of each run, Pallas kernels for 0% -> 66%
where the time goes in v1:
time: 380 us; the launch traced here: 378 us
  Pallas kernels  250 us (66%)
  local copies, waits for them, and re-layouts  67.3 us (18%)
  other arithmetic  47.2 us (12%)
  between operations  14.3 us (4%)
    pallas_call x1, Pallas kernels, moe(): pl.pallas_call(functools.partial(moe_kernel, side), out_shape=jax.ShapeDt...  250 us
    another operation x5, other arithmetic, body(): new_w = tuple((jnp.stack([p[i] for p in placed]) for i in range(3)))  31 us
    gather x6, local copies, waits for them, and re-layouts, send_moved(): jnp.take(weight_arr, local_idx, axis=0)  24.3 us
    gather x6, local copies, waits for them, and re-layouts, place_moved(): jnp.take(arrived_arr, pick_idx, axis=0)  22.5 us
    squeeze x3, local copies, waits for them, and re-layouts, body(): layer_w = (w_gate[layer], w_up[layer], w_down[layer])  15.2 us
    select_n x4, other arithmetic, send_moved(): jnp.where(is_source[:, None, None], jnp.take(weight_arr, local_idx, axis=...  13.1 us
  transfers between devices with their start and end apart: 1, of which 0 were waited for; matrix products, arithmetic and copies ran while one was open for 1% of the time, Pallas kernels for 66%

profile of v1, /device:TPU:98, one launch (start us, length us, event | category | flops | bytes accessed | tf_op | source)
XLA Modules:
  0.0 378.5 jit_solution(379028865713650873)
XLA Ops:
  7.2 0.1 all-reduce.3.cloned.1.call-start
  7.2 0.8 slice_bitcast_fusion.11
  8.0 0.8 slice_bitcast_fusion.8
  8.8 0.2 fusion.10
  9.0 0.0 slice-start.2
  9.0 0.0 slice-start.3
  9.0 6.2 %slice_bitcast_fusion.5 = (bf16[2,1536,512]{2,1,0:T(8,128)(2,1)}, bf16[2,1536,512]{2,1,0:T(8,128)(2,1)}) fusion(bf16[2,2,1536,512]{3,2,1,0:T(8,128)(2,1)} %wg.1), kind=kLoop, calls=%fused_computation.38 | loop fusion | bytes 12582912 | tf_op jit(solution)/shard_map/squeeze | solution.py:340
  15.2 0.0 slice-done.2
  15.2 0.0 slice-done.3
  15.2 3.1 slice_bitcast_fusion.3
  18.3 2.6 gather_fusion
  21.0 4.3 %gather_fusion.4 = bf16[2,1536,512]{2,1,0:T(8,128)(2,1)} fusion(bf16[2,1536,512]{2,1,0:T(8,128)(2,1)} %get-tuple-element.30, s32[1024]{0:T(1024)S(1)} %pad_clamp_fusion.3), kind=kCustom, calls=%fused_computation.5.clone | custom fusion | bytes 6291464 | tf_op jit(solution)/shard_map/jit(_take)/gather | solution.py:26
  25.3 4.3 %gather_fusion.2 = bf16[2,1536,512]{2,1,0:T(8,128)(2,1)} fusion(bf16[2,1536,512]{2,1,0:T(8,128)(2,1)} %get-tuple-element.33, s32[1024]{0:T(1024)S(1)} %pad_clamp_fusion.1), kind=kCustom, calls=%fused_computation.3.clone | custom fusion | bytes 6291464 | tf_op jit(solution)/shard_map/jit(_take)/gather | solution.py:26
  29.6 4.3 %gather_fusion.6 = bf16[2,1536,512]{2,1,0:T(8,128)(2,1)} fusion(bf16[2,1536,512]{2,1,0:T(8,128)(2,1)} %get-tuple-element.31, s32[1024]{0:T(1024)S(1)} %pad_clamp_fusion.1), kind=kCustom, calls=%fused_computation.7.clone | custom fusion | bytes 6291464 | tf_op jit(solution)/shard_map/jit(_take)/gather | solution.py:26
  33.9 6.0 %slice_bitcast_fusion.1 = (bf16[2,512,1536]{2,1,0:T(8,128)(2,1)}, bf16[2,512,1536]{2,1,0:T(8,128)(2,1)}) fusion(bf16[2,2,512,1536]{3,2,1,0:T(8,128)(2,1)} %wd.1), kind=kLoop, calls=%fused_computation.34 | loop fusion | bytes 12582912 | tf_op jit(solution)/shard_map/squeeze | solution.py:340
  39.9 4.3 %gather_fusion.10 = bf16[2,512,1536]{2,1,0:T(8,128)(2,1)} fusion(bf16[2,512,1536]{2,1,0:T(8,128)(2,1)} %get-tuple-element.29, s32[1024]{0:T(1024)S(1)} %pad_clamp_fusion.1), kind=kCustom, calls=%fused_computation.10.clone | custom fusion | bytes 6291464 | tf_op jit(solution)/shard_map/jit(_take)/gather | solution.py:26
  44.2 4.4 %gather_fusion.8 = bf16[2,512,1536]{2,1,0:T(8,128)(2,1)} fusion(bf16[2,512,1536]{2,1,0:T(8,128)(2,1)} %get-tuple-element.28, s32[1024]{0:T(1024)S(1)} %pad_clamp_fusion.3), kind=kCustom, calls=%fused_computation.1.clone | custom fusion | bytes 6291464 | tf_op jit(solution)/shard_map/jit(_take)/gather | solution.py:26
  48.6 0.0 copy-start.4
  48.6 4.2 %select_select_fusion.3 = bf16[2,512,1536]{2,1,0:T(8,128)(2,1)} fusion(bf16[2,512,1536]{2,1,0:T(8,128)(2,1)} %gather_fusion.8, pred[2]{0:T(512)(128)(4,1)S(1)} %get-tuple-element.18, pred[2]{0:T(512)(128)(4,1)S(1)} %get-tuple-element.50), kind=kLoop, calls=%fused_computation.20 | loop fusion | flops 3145728 | bytes 6291460 | tf_op jit(solution)/shard_map/jit(_where)/select_n | solution.py:26
  52.8 0.0 copy-done.4
  52.8 0.0 copy-start.7
  52.8 3.3 select_select_fusion.7
  56.1 0.0 copy-done.7
  56.1 0.0 copy-start.5
  56.1 0.0 copy-start.6
  56.1 2.2 select_select_fusion.1
  58.3 0.9 copy-done.5
  59.2 1.0 copy-done.6
  60.1 3.4 select_select_fusion.5
  63.6 0.0 copy-start.11
  63.6 0.1 all-reduce.3.cloned.1.call-update
  63.6 0.2 select_reduce_fusion.2
  63.8 0.4 copy-done.11
  64.3 0.0 copy-done.12
  64.3 0.2 select_reduce_fusion.1
  64.5 0.2 select_reduce_fusion
  64.7 0.7 pad_maximum_fusion.3.coef
  65.4 249.6 %moe_rings.1 = bf16[64,1536]{1,0:T(8,128)(2,1)} custom-call(bf16[64,1536]{1,0:T(8,128)(2,1)} %tok.1, f32[64,128]{1,0:T(8,128)} %pad_maximum_fusion.3.coef, bf16[2,2,1536,512]{3,2,1,0:T(8,128)(2,1)} %wg.1, bf16[2,2,1536,512]{3,2,1,0:T(8,128)(2,1)} %wu.1, bf16[2,2,512,1536]{3,2,1,0:T(8,128)(2,1)} %wd.1, bf16[2,1536,1024]{2,1,0:T(8,128)(2,1)} %sg.1, ...), custom_call_target="tpu_custom_call" | custom-call | flops 159450660864 | bytes 41943040 | tf_op jit(solution)/shard_map/moe_rings/pallas_call | solution.py:320
  315.0 0.8 slice_bitcast_fusion.9
  315.7 0.7 fusion.6
  316.4 0.7 fusion.8
  317.1 0.2 fusion.7
  317.4 0.0 all-reduce.3.cloned.1.call-done
  317.4 4.3 %gather_fusion.11 = bf16[2,512,1536]{2,1,0:T(8,128)(2,1)} fusion(bf16[2,512,1536]{2,1,0:T(8,128)(2,1)} %get-tuple-element.16, s32[1024]{0:T(1024)S(1)} %pad_clamp_fusion), kind=kCustom, calls=%fused_computation.11.clone | custom fusion | bytes 6291464 | tf_op jit(solution)/shard_map/jit(_take)/gather | solution.py:34
  321.7 4.4 %gather_fusion.3 = bf16[2,1536,512]{2,1,0:T(8,128)(2,1)} fusion(bf16[2,1536,512]{2,1,0:T(8,128)(2,1)} %get-tuple-element.12, s32[1024]{0:T(1024)S(1)} %pad_clamp_fusion), kind=kCustom, calls=%fused_computation.4.clone | custom fusion | bytes 6291464 | tf_op jit(solution)/shard_map/jit(_take)/gather | solution.py:34
  326.2 0.0 copy-done.9
  326.2 2.4 gather_fusion.9
  328.6 4.4 %gather_fusion.5 = bf16[2,1536,512]{2,1,0:T(8,128)(2,1)} fusion(bf16[2,1536,512]{2,1,0:T(8,128)(2,1)} %get-tuple-element.15, s32[1024]{0:T(1024)S(1)} %pad_clamp_fusion.2), kind=kCustom, calls=%fused_computation.6.clone | custom fusion | bytes 6291464 | tf_op jit(solution)/shard_map/jit(_take)/gather | solution.py:34
  333.0 0.0 copy-done.8
  333.0 2.4 gather_fusion.7
  335.4 4.4 %gather_fusion.1 = bf16[2,1536,512]{2,1,0:T(8,128)(2,1)} fusion(bf16[2,1536,512]{2,1,0:T(8,128)(2,1)} %get-tuple-element.13, s32[1024]{0:T(1024)S(1)} %pad_clamp_fusion.2), kind=kCustom, calls=%fused_computation.2.clone | custom fusion | bytes 6291464 | tf_op jit(solution)/shard_map/jit(_take)/gather | solution.py:34
  339.9 6.9 %fusion.1 = (bf16[1,2,512,1536]{3,2,1,0:T(8,128)(2,1)S(1)}, bf16[1,2,512,1536]{3,2,1,0:T(8,128)(2,1)}) fusion(bf16[2,512,1536]{2,1,0:T(8,128)(2,1)} %gather_fusion.9, pred[2]{0:T(512)(128)(4,1)S(1)} %get-tuple-element.63, pred[2]{0:T(512)(128)(4,1)S(1)} %get-tuple-element.61, bf16[2,2,512,1536]{3,2,1,0:T(8,128)(2,1)} %wd.1, ...), kind=kLoop, calls=%fused_computation.19 | loop fusion | flops 6291456 | bytes 18874376 | tf_op jit(solution)/shard_map/stack | solution.py:346
  346.8 5.3 %pad_maximum_fusion.2 = bf16[2,2,512,1536]{3,2,1,0:T(8,128)(2,1)} fusion(bf16[1,2,512,1536]{3,2,1,0:T(8,128)(2,1)} %get-tuple-element.23, bf16[1,2,512,1536]{3,2,1,0:T(8,128)(2,1)S(1)} %get-tuple-element.22), kind=kLoop, calls=%fused_computation.14 | loop fusion | flops 3145728 | bytes 12582912 | tf_op jit(solution)/shard_map/stack | solution.py:346
  352.1 0.0 slice-done
  352.1 0.0 slice-done.1
  352.1 0.0 copy-done
  352.1 0.0 copy-done.1
  352.2 9.2 %fusion.5 = (bf16[1,2,1536,512]{3,2,1,0:T(8,128)(2,1)}, bf16[1,2,1536,512]{3,2,1,0:T(8,128)(2,1)}, bf16[1,2,1536,512]{3,2,1,0:T(8,128)(2,1)}, bf16[1,2,1536,512]{3,2,1,0:T(8,128)(2,1)}) fusion(bf16[2,1536,512]{2,1,0:T(8,128)(2,1)} %gather_fusion.1, pred[2]{0:T(512)(128)(4,1)S(1)} %get-tuple-element.63, pred[2]{0:T(512)(128)(4,1)S(1)} %get-tuple-element.61, ...), kind=kLoop, calls=%fused_computation.31 | loop fusion | flops 12582912 | bytes 37748744 | tf_op jit(solution)/shard_map/stack | solution.py:346
  361.4 6.3 %pad_maximum_fusion.1 = bf16[2,2,1536,512]{3,2,1,0:T(8,128)(2,1)} fusion(bf16[1,2,1536,512]{3,2,1,0:T(8,128)(2,1)} %get-tuple-element.38, bf16[1,2,1536,512]{3,2,1,0:T(8,128)(2,1)} %get-tuple-element.39), kind=kLoop, calls=%fused_computation.13 | loop fusion | flops 3145728 | bytes 12582912 | tf_op jit(solution)/shard_map/stack | solution.py:346
  367.7 0.0 copy-done.2
  367.7 0.0 copy-done.3
  367.7 3.2 pad_maximum_fusion
  370.9 0.0 copy-done.10
  370.9 0.7 copy.47
  (29 shorter events, 0.1 us)
Async XLA Ops:
  7.2 310.2 %all-reduce.3.cloned.1.call-start = ((), (), s32[]{:S(2)}) async-start(), calls=%async_computation | async-start | bytes 37748736 | tf_op jit(solution)/shard_map/psum | solution.py:342
  9.0 6.2 %slice-start.2 = ((s8[6291456]{0:T(1024)(128)(4,1)}), s8[4194304]{0:T(1024)(128)(4,1)S(1)}, s32[]{:S(2)}) async-start(s8[6291456]{0:T(1024)(128)(4,1)} %bitcast.58), calls=%async_computation.3 | async-start | bytes 8388608
  9.0 6.2 %slice-start.3 = ((s8[6291456]{0:T(1024)(128)(4,1)}), s8[2097152]{0:T(1024)(128)(4,1)S(1)}, s32[]{:S(2)}) async-start(s8[6291456]{0:T(1024)(128)(4,1)} %bitcast.58), calls=%async_computation.4 | async-start | bytes 4194304
  48.6 4.2 %copy-start.4 = (bf16[2,1536,512]{2,1,0:T(8,128)(2,1)S(1)}, bf16[2,1536,512]{2,1,0:T(8,128)(2,1)}, u32[]{:S(2)}) copy-start(bf16[2,1536,512]{2,1,0:T(8,128)(2,1)} %gather_fusion.4) | copy-start | bytes 9437188
  52.8 3.3 copy-start.7
  56.1 3.0 copy-start.5
  56.1 4.0 %copy-start.6 = (bf16[2,1536,512]{2,1,0:T(8,128)(2,1)S(1)}, bf16[2,1536,512]{2,1,0:T(8,128)(2,1)}, u32[]{:S(2)}) copy-start(bf16[2,1536,512]{2,1,0:T(8,128)(2,1)} %gather_fusion.6) | copy-start | bytes 9437188
  63.6 0.7 copy-start.11
  63.6 0.7 copy-start.12
  321.7 4.5 %copy-start.9 = (bf16[2,512,1536]{2,1,0:T(8,128)(2,1)S(1)}, bf16[2,512,1536]{2,1,0:T(8,128)(2,1)}, u32[]{:S(2)}) copy-start(bf16[2,512,1536]{2,1,0:T(8,128)(2,1)} %get-tuple-element.17) | copy-start | bytes 9437188
  328.6 4.4 %copy-start.8 = (bf16[2,1536,512]{2,1,0:T(8,128)(2,1)S(1)}, bf16[2,1536,512]{2,1,0:T(8,128)(2,1)}, u32[]{:S(2)}) copy-start(bf16[2,1536,512]{2,1,0:T(8,128)(2,1)} %get-tuple-element.14) | copy-start | bytes 9437188
  335.4 16.7 %slice-start = ((s8[6291456]{0:T(1024)(128)(4,1)}), s8[2097152]{0:T(1024)(128)(4,1)S(1)}, s32[]{:S(2)}) async-start(s8[6291456]{0:T(1024)(128)(4,1)} %bitcast.56), calls=%async_computation.1 | async-start | bytes 4194304
  339.9 12.3 %slice-start.1 = ((s8[6291456]{0:T(1024)(128)(4,1)}), s8[4194304]{0:T(1024)(128)(4,1)S(1)}, s32[]{:S(2)}) async-start(s8[6291456]{0:T(1024)(128)(4,1)} %bitcast.56), calls=%async_computation.2 | async-start | bytes 8388608
  346.8 5.3 %copy-start = (bf16[2,1536,512]{2,1,0:T(8,128)(2,1)S(1)}, bf16[2,1536,512]{2,1,0:T(8,128)(2,1)}, u32[]{:S(2)}) copy-start(bf16[2,1536,512]{2,1,0:T(8,128)(2,1)} %gather_fusion.3) | copy-start | bytes 9437188
  346.8 5.3 %copy-start.1 = (bf16[2,1536,512]{2,1,0:T(8,128)(2,1)S(1)}, bf16[2,1536,512]{2,1,0:T(8,128)(2,1)}, u32[]{:S(2)}) copy-start(bf16[2,1536,512]{2,1,0:T(8,128)(2,1)} %gather_fusion.5) | copy-start | bytes 9437188
  361.4 6.3 %copy-start.2 = (bf16[1,2,1536,512]{3,2,1,0:T(8,128)(2,1)S(1)}, bf16[1,2,1536,512]{3,2,1,0:T(8,128)(2,1)}, u32[]{:S(2)}) copy-start(bf16[1,2,1536,512]{3,2,1,0:T(8,128)(2,1)} %get-tuple-element.26) | copy-start | bytes 9437188
  361.4 6.3 %copy-start.3 = (bf16[1,2,1536,512]{3,2,1,0:T(8,128)(2,1)S(1)}, bf16[1,2,1536,512]{3,2,1,0:T(8,128)(2,1)}, u32[]{:S(2)}) copy-start(bf16[1,2,1536,512]{3,2,1,0:T(8,128)(2,1)} %get-tuple-element.27) | copy-start | bytes 9437188
  367.7 3.3 copy-start.10
Sparse Core Ops, SparseCore 0:
  63.8 229.8 all-reduce.2

commit v2 on v1

--- a/solution.py
+++ b/solution.py
@@ -17,21 +17,6 @@
     slot_ids = jnp.arange(slot_map.shape[0], dtype=jnp.int32)
     hit_mask = slot_map[None, :] == wanted[:, None]
     return jnp.min(jnp.where(hit_mask, slot_ids[None, :], slot_map.shape[0]), axis=1)
-
-
-def send_moved(weights, slot_map, move_expert, slots_dev, my_dev):
-    source = first_holder(slot_map, move_expert)
-    is_source = (source // slots_dev) == my_dev
-    local_idx = source % slots_dev
-    return tuple(jnp.where(is_source[:, None, None], jnp.take(weight_arr, local_idx, axis=0), jnp.zeros((), weight_arr.dtype)) for weight_arr in weights)
-
-
-def place_moved(weights, arrived, move_slot, slots_dev, my_dev):
-    local_ids = my_dev * slots_dev + jnp.arange(slots_dev, dtype=jnp.int32)
-    match_mask = (move_slot[None, :] == local_ids[:, None]).astype(jnp.int32)
-    is_target = jnp.max(match_mask, axis=1) > 0
-    pick_idx = jnp.argmax(match_mask, axis=1)
-    return tuple(jnp.where(is_target[:, None, None], jnp.take(arrived_arr, pick_idx, axis=0), weight_arr) for arrived_arr, weight_arr in zip(arrived, weights))
 
 
 def gate_table(routes, gate_vals, old_map):
@@ -44,10 +29,20 @@
     return jnp.concatenate(cols, axis=1)
 
 
-def moe_kernel(side, tok, coef, wg, wu, wd, sg, su, sd, out,
-               xb, cb, wgv, wuv, wdv, sgv, suv, sdv, act, hacc, own, pcs, pcr, rs,
+SUB = 32
+CELLS = 4
+
+
+def unit_counts(dim, ff):
+    per_block, blocks = ff // 4 // SUB, dim // ff
+    return per_block, blocks, 3 * blocks * per_block
+
+
+def moe_kernel(side, src, tok, coef, wg, wu, wd, sg, su, sd, out, hist,
+               cell, obuf, cin, cout, xb, cb, wgv, wuv, wdv, sgv, suv, sdv, act, hacc, own, pcs, pcr, rs,
                wsem, ssem, tsem, xsend, xrecv, msend, mrecv, csend, crecv, cmsend, cmrecv,
-               psend, precv, rsend, rrecv, mid):
+               psend, precv, rsend, rrecv,
+               osend, orecv, hsend, hlocal, hrecv, vsend, vrecv, cred, vcred, mid):
     layers, slots, dim, ff = wg.shape
     rows = tok.shape[0]
     half = rows // 2
@@ -99,6 +94,122 @@
     def rcopy(l, s, d):
         return remote(rs.at[s, part(d)], rs.at[s + 1, part(d)], rsend.at[l, s, d], rrecv.at[l, s + 1, d], peers[d])
 
+    per_block, blocks, units = unit_counts(dim, ff)
+    per_matrix = blocks * per_block
+    total_moves = src.shape[0]
+    per_layer = total_moves // layers
+    trips = units + n - 1
+    quarter = ff // 4
+
+    def ocopy(t, d):
+        return remote(obuf.at[lax.rem(t, 2), d], cell.at[lax.rem(t, CELLS), d], osend.at[lax.rem(t, 2), d], orecv.at[lax.rem(t, CELLS), d], peers[d])
+
+    def hcopy(t):
+        return remote(cell.at[lax.rem(t, CELLS)], hist.at[1, t], hsend.at[lax.rem(t, 2)], hrecv.at[t], mate)
+
+    def hkeep(t):
+        return pltpu.make_async_copy(cell.at[lax.rem(t, CELLS)], hist.at[0, t], hlocal.at[lax.rem(t, 2)])
+
+    def vcopy(t):
+        return remote(cout.at[lax.rem(t, 2)], cin.at[lax.rem(t, 2)], vsend.at[lax.rem(t, 2)], vrecv.at[lax.rem(t, 2)], mate)
+
+    def own_piece(m, t, mv, q):
+        j = t - m * per_matrix
+        b = lax.div(j, per_block)
+        r = q * quarter + lax.rem(j, per_block) * SUB
+        l = mv // per_layer
+        val = None
+        for i in range(slots):
+            if m < 2:
+                new = (wgv, wuv)[m][l, i, pl.ds(pl.multiple_of(b * ff + r, SUB), SUB), :]
+            else:
+                new = wdv[l, i, pl.ds(pl.multiple_of(r, SUB), SUB), pl.ds(pl.multiple_of(b * ff, ff), ff)]
+            val = new if val is None else jnp.where(src[mv] == me * slots + i, new, val)
+        return val
+
+    def by_matrix(t, fn):
+        for m in range(3):
+            @pl.when((t >= m * per_matrix) & (t < (m + 1) * per_matrix))
+            def _():
+                fn(m)
+
+    def offer(t):
+        slot = lax.rem(t, 2)
+
+        @pl.when(t >= 2)
+        def _():
+            vcopy(t - 2).wait_send()
+            pl.semaphore_wait(vcred, 1)
+
+        def fill(m):
+            for d in range(2):
+                for mv in range(total_moves):
+                    cout[slot, d, mv] = own_piece(m, t, mv, 2 * (1 - core) + d)
+
+        by_matrix(t, fill)
+        vcopy(t).start()
+
+    def convey(t):
+        last = lax.rem(t + CELLS - 1, CELLS)
+        slot = lax.rem(t, 2)
+
+        @pl.when((t >= 2) & (t <= trips + 1))
+        def _():
+            hkeep(t - 2).wait()
+            hcopy(t - 2).wait_send()
+
+        @pl.when((t >= 1) & (t <= trips + 1 - CELLS))
+        def _():
+            for d in range(2):
+                pl.semaphore_signal(cred.at[d], inc=1, device_id={'ep': peers[1 - d]}, device_id_type=MESH)
+
+        @pl.when((t >= 1) & (t <= trips))
+        def _():
+            for d in range(2):
+                ocopy(t - 1, d).wait_recv()
+            hkeep(t - 1).start()
+            hcopy(t - 1).start()
+
+        @pl.when(t < trips)
+        def _():
+            @pl.when(t >= CELLS - 1)
+            def _():
+                for d in range(2):
+                    pl.semaphore_wait(cred.at[d], 1)
+
+            @pl.when(t >= 2)
+            def _():
+                for d in range(2):
+                    ocopy(t - 2, d).wait_send()
+
+            @pl.when(t < units)
+            def _():
+                vcopy(t).wait_recv()
+
+                def fill(m):
+                    for d in range(2):
+                        for mv in range(total_moves):
+                            holder = lax.div(src[mv], slots)
+                            val = jnp.where(holder == mate, cin[slot, d, mv], cell[last, d, mv])
+                            obuf[slot, d, mv] = jnp.where(holder == me, own_piece(m, t, mv, 2 * core + d), val)
+
+                by_matrix(t, fill)
+
+                @pl.when(t < units - 2)
+                def _():
+                    pl.semaphore_signal(vcred, inc=1, device_id={'ep': mate}, device_id_type=MESH)
+
+            @pl.when(t >= units)
+            def _():
+                obuf[slot] = cell[last]
+
+            for d in range(2):
+                ocopy(t, d).start()
+
+            @pl.when(t + 1 < units)
+            def _():
+                offer(t + 1)
+
     def shared_loads(l):
         return [pltpu.make_async_copy(src.at[l], dst, ssem.at[l, i]) for i, (src, dst) in enumerate(((sg, sgv), (su, suv), (sd, sdv)))]
 
@@ -114,6 +225,8 @@
     for l in range(layers):
         for copy in expert_loads(l):
             copy.start()
+
+    cell[CELLS - 1] = jnp.zeros(cell.shape[1:], cell.dtype)
 
     barrier = pltpu.get_barrier_semaphore()
     for dev in peers + (mate,):
@@ -193,8 +306,11 @@
         if l + 1 < layers:
             for copy in shared_loads(l + 1):
                 copy.start()
-        for copy in expert_loads(l):
-            copy.wait()
+        if l == 0:
+            for k in range(layers):
+                for copy in expert_loads(k):
+                    copy.wait()
+            offer(0)
         if l > 0:
             pl.semaphore_wait(mid, 3)
         wait_mate(l, 0)
@@ -206,6 +322,8 @@
         to_mate(l, 1)
 
         def step(s, carry):
+            trip = 2 * (l * (n - 1) + s - 1)
+            convey(trip)
             wait_mate(l, s)
 
             @pl.when(s >= 2)
@@ -224,6 +342,7 @@
             def _():
                 forward(l, s + 1)
 
+            convey(trip + 1)
             pcopy(l, s).wait_recv()
 
             @pl.when(s == 1)
@@ -279,9 +398,100 @@
             lax.fori_loop(1, n, one, 0)
 
     drain(layers - 1)
-
-
-def moe(tok, coef, wg, wu, wd, sg, su, sd, group):
+    for t in (trips - 2, trips - 1):
+        for d in range(2):
+            ocopy(t, d).wait_send()
+    for t in (units - 2, units - 1):
+        vcopy(t).wait_send()
+
+    def landed(t, carry):
+        hcopy(t).wait_recv()
+        return carry
+
+    lax.fori_loop(0, trips, landed, 0)
+
+
+def place_kernel(side, src, slot_to, hist, wg, wu, wd, og, ou, od, bg, bu, bd, rsem, wsem):
+    layers, slots = wg.shape[:2]
+    n = side * side
+    per_layer = src.shape[0] // layers
+    ff = hist.shape[-1]
+    per_block = ff // 4 // SUB
+    blocks = wg.shape[2] // (4 * per_block)
+    me = lax.axis_index('ep')
+
+    def place(dev):
+        chip = lax.div(dev, 2)
+        y, x = lax.div(chip, side), lax.rem(chip, side)
+        turn = lax.rem(x + y, side)
+        return side * y + turn, side * x + turn
+
+    core = lax.rem(me, 2)
+    at = place(me)
+    groups = tuple(zip((wg, wu, wd), (bg, bu, bd), (og, ou, od)))
+    for l in range(layers):
+        for i in range(slots):
+            here = me * slots + i
+            moved = slot_to[l * per_layer] == here
+            mv = l * per_layer
+            for k in range(1, per_layer):
+                hit = slot_to[l * per_layer + k] == here
+                moved = moved | hit
+                mv = jnp.where(hit, l * per_layer + k, mv)
+            origin = place(lax.div(src[mv], slots))
+
+            @pl.when(jnp.logical_not(moved))
+            def _():
+                for m, (w, buf, _) in enumerate(groups):
+                    pltpu.make_async_copy(w.at[l, i], buf.at[l, i], rsem.at[l, i, m]).start()
+
+            @pl.when(moved)
+            def _():
+                for which in range(2):
+                    ring = core if which == 0 else 1 - core
+                    gap = (at[0] - origin[0]) * (1 - ring) + (at[1] - origin[1]) * ring
+                    for d in range(2):
+                        away = lax.rem((gap if d == 0 else -gap) - 1 + 2 * n, n)
+                        for m, (_, buf, _) in enumerate(groups):
+                            for b in range(blocks):
+                                first = away + (m * blocks + b) * per_block
+                                come = hist.at[which, pl.ds(first, per_block), d, mv]
+                                q = (2 * ring + d) * per_block
+                                if m < 2:
+                                    dst = buf.at[l, i, pl.ds(b * 4 * per_block + q, per_block)]
+                                else:
+                                    dst = buf.at[l, i, pl.ds(q, per_block), :, pl.ds(b * ff, ff)]
+                                pltpu.make_async_copy(come, dst, rsem.at[l, i, m]).start()
+
+    for l in range(layers):
+        for i in range(slots):
+            for m, (w, buf, o) in enumerate(groups):
+                pltpu.make_async_copy(w.at[l, i], buf.at[l, i], rsem.at[l, i, m]).wait()
+                pltpu.make_async_copy(buf.at[l, i], o.at[l, i], wsem.at[l, i, m]).start()
+    for l in range(layers):
+        for i in range(slots):
+            for m, (w, buf, o) in enumerate(groups):
+                pltpu.make_async_copy(buf.at[l, i], o.at[l, i], wsem.at[l, i, m]).wait()
+
+
+def place_weights(src, slot_to, hist, weights, side):
+    layers, slots = weights[0].shape[:2]
+    split = [w.reshape(layers, slots, w.shape[2] // SUB, SUB, w.shape[3]) for w in weights]
+    any_spec = pl.BlockSpec(memory_space=pl.ANY)
+    smem = pl.BlockSpec(memory_space=pltpu.SMEM)
+    out = pl.pallas_call(
+        functools.partial(place_kernel, side),
+        out_shape=[jax.ShapeDtypeStruct(w.shape, w.dtype) for w in split],
+        in_specs=[smem, smem] + [any_spec] * 4,
+        out_specs=[any_spec] * 3,
+        scratch_shapes=[pltpu.VMEM(w.shape, w.dtype) for w in split] + [pltpu.SemaphoreType.DMA((layers, slots, 3))] * 2,
+        compiler_params=pltpu.CompilerParams(vmem_limit_bytes=40 << 20),
+        name='place_slots',
+    )(src, slot_to, hist, *split)
+    return tuple(o.reshape(w.shape) for o, w in zip(out, weights))
+
+
+def moe(src, tok, coef, wg, wu, wd, sg, su, sd, group):
     layers, slots, dim, ff = wg.shape
     rows = tok.shape[0]
     sff = sg.shape[2]
@@ -292,7 +502,16 @@
     any_spec = pl.BlockSpec(memory_space=pl.ANY)
     vmem = pltpu.VMEM
     act_n = max(slots, -(-sff // ff))
+    per_block, blocks, units = unit_counts(dim, ff)
+    trips = units + n - 1
+    moves = src.shape[0]
+    assert 2 * layers * (n - 1) > trips + 1 and units > 2
+    piece = (2, moves, SUB, ff)
     scratch = [
+        vmem((CELLS,) + piece, BF16),
+        vmem((2,) + piece, BF16),
+        vmem((2,) + piece, BF16),
+        vmem((2,) + piece, BF16),
         vmem((layers, n, 2 * rows, dim), BF16),
         vmem((n, 2 * rows, coef.shape[1]), F32),
         vmem((layers, slots, dim, ff), BF16),
@@ -314,36 +533,33 @@
         dma((n,)), dma((n,)),
         dma((2,)), dma((layers, n)),
         dma((layers, n, 2)), dma((layers, n + 1, 2)),
+        dma((2, 2)), dma((CELLS, 2)), dma((2,)), dma((2,)), dma((trips,)), dma((2,)), dma((2,)),
+        pltpu.SemaphoreType.REGULAR((2,)), pltpu.SemaphoreType.REGULAR,
         pltpu.SemaphoreType.REGULAR,
     ]
     flops = layers * 2 * 3 * dim * (ff * slots * rows * group + sff * rows)
     return pl.pallas_call(
         functools.partial(moe_kernel, side),
-        out_shape=jax.ShapeDtypeStruct((rows, dim), BF16),
-        in_specs=[any_spec] * 8,
-        out_specs=pl.BlockSpec(memory_space=pltpu.VMEM),
+        out_shape=[jax.ShapeDtypeStruct((rows, dim), BF16), jax.ShapeDtypeStruct((2, trips) + piece, BF16)],
+        in_specs=[pl.BlockSpec(memory_space=pltpu.SMEM)] + [any_spec] * 8,
+        out_specs=[pl.BlockSpec(memory_space=pltpu.VMEM), any_spec],
         scratch_shapes=scratch,
         compiler_params=pltpu.CompilerParams(collective_id=0, has_side_effects=True, vmem_limit_bytes=67043328),
         cost_estimate=pl.CostEstimate(flops=flops * 4, bytes_accessed=40 << 20, transcendentals=0),
         name='moe_rings',
-    )(tok, coef, wg, wu, wd, sg, su, sd)
+    )(src, tok, coef, wg, wu, wd, sg, su, sd)
 
 
 def solution(mesh):
     group = mesh.shape['ep']
 
     def body(tok_in, routes, gate_vals, w_gate, w_up, w_down, sh_gate, sh_up, sh_down, old_map, move_slot, move_expert):
-        my_dev = lax.axis_index('ep')
-        layers, slots_dev = w_gate.shape[:2]
-        placed = []
-        for layer in range(layers):
-            layer_w = (w_gate[layer], w_up[layer], w_down[layer])
-            outgoing = send_moved(layer_w, old_map[layer], move_expert[layer], slots_dev, my_dev)
-            arrived = lax.psum(outgoing, 'ep')
-            placed.append(place_moved(layer_w, arrived, move_slot[layer], slots_dev, my_dev))
+        layers = w_gate.shape[0]
+        src = jnp.concatenate([first_holder(old_map[l], move_expert[l]) for l in range(layers)])
         coef = gate_table(routes, gate_vals, old_map)
-        hidden = moe(tok_in, coef, w_gate, w_up, w_down, sh_gate, sh_up, sh_down, group)
-        new_w = tuple(jnp.stack([p[i] for p in placed]) for i in range(3))
+        hidden, hist = moe(src, tok_in, coef, w_gate, w_up, w_down, sh_gate, sh_up, sh_down, group)
+        side = int(round((group // 2) ** 0.5))
+        new_w = place_weights(src, move_slot.reshape(-1), hist, (w_gate, w_up, w_down), side)
         return (hidden,) + new_w
 
     weight_spec = P(None, TOKEN_AXES, None, None)

time: 380 us -> 319 us (0.84)
  local copies, waits for them, and re-layouts: 67.3 us -> 11.9 us
  Pallas kernels: 250 us -> 304 us
  other arithmetic: 47.2 us -> 2.14 us
  between operations: 14.3 us -> 0.72 us
    pallas_call x1 -> x2, Pallas kernels: 250 us -> 304 us  [the longest x1 294 us: moe(): pl.pallas_call(functools.partial(moe_kernel, side), out_shape=[jax.ShapeD...]
    gather x12 -> x0, local copies, waits for them, and re-layouts: 46.8 us -> none  [the longest x6 24.3 us: send_moved(): jnp.take(weight_arr, local_idx, axis=0)]
    another operation x7 -> x0, other arithmetic: 32.4 us -> none  [the longest x5 31 us: body(): new_w = tuple((jnp.stack([p[i] for p in placed]) for i in range(3)))]
    squeeze x3 -> x0, local copies, waits for them, and re-layouts: 15.2 us -> none  [body(): layer_w = (w_gate[layer], w_up[layer], w_down[layer])]
    select_n x6 -> x0, other arithmetic: 13.1 us -> none  [the longest x4 13.1 us: send_moved(): jnp.where(is_source[:, None, None], jnp.take(weight_arr, local_idx, axis=...]
    unnamed x35 -> x15, local copies, waits for them, and re-layouts: 2.99 us -> 7.58 us
  transfers between devices with their start and end apart: 1 -> 0, of which waited for: 0 -> 0; matrix products, arithmetic and copies ran while one was open for 1% -> 0% of each run, Pallas kernels for 66% -> 0%
where the time goes in v2:
time: 319 us
  Pallas kernels  304 us (95%)
  local copies, waits for them, and re-layouts  11.9 us (4%)
    pallas_call x1, Pallas kernels, moe(): pl.pallas_call(functools.partial(moe_kernel, side), out_shape=[jax.ShapeD...  294 us
    pallas_call x1, Pallas kernels, place_weights(): pl.pallas_call(functools.partial(place_kernel, side), out_shape=[jax.Shap...  10.3 us
    unnamed x15, local copies, waits for them, and re-layouts  7.58 us

profile of v2, /device:TPU:98, one launch (start us, length us, event | category | flops | bytes accessed | tf_op | source)
XLA Modules:
  0.0 319.0 jit_solution(3996302269745238312)
XLA Ops:
  0.6 1.3 reshape.51.slot_to
  1.9 0.8 slice_bitcast_fusion.3
  2.7 0.2 select_reduce_fusion.3
  2.8 0.2 select_reduce_fusion.2
  3.0 0.8 slice_bitcast_fusion.2
  3.8 0.2 fusion
  4.0 0.6 pad_add_fusion.src
  4.6 0.8 fusion.2
  5.4 0.8 fusion.3
  6.2 0.3 select_reduce_fusion
  6.5 0.7 pad_maximum_fusion.coef
  7.2 293.9 %moe_rings.1 = (bf16[64,1536]{1,0:T(8,128)(2,1)}, bf16[2,51,2,4,32,512]{5,4,3,2,1,0:T(8,128)(2,1)}) custom-call(s32[4]{0:T(128)} %pad_add_fusion.src, bf16[64,1536]{1,0:T(8,128)(2,1)} %tok.1, f32[64,128]{1,0:T(8,128)} %pad_maximum_fusion.coef, bf16[2,2,1536,512]{3,2,1,0:T(8,128)(2,1)} %wg.1, bf16[2,2,1536,512]{3,2,1,0:T(8,128)(2,1)} %wu.1, ...), custom_call_target="tpu_custom_call" | custom-call | flops 159450660864 | bytes 41943040 | tf_op jit(solution)/shard_map/moe_rings/pallas_call | solution.py:541
  301.1 0.0 copy-start
  301.1 2.8 copy-done
  303.9 0.0 copy-start.1
  303.9 2.8 copy-done.1
  306.7 0.0 copy-start.2
  306.7 0.7 copy-done.2
  307.3 0.0 copy-start.3
  307.3 0.7 copy-done.3
  308.0 0.0 copy-start.4
  308.0 10.3 %place_slots.1 = (bf16[2,2,48,32,512]{4,3,2,1,0:T(8,128)(2,1)}, bf16[2,2,48,32,512]{4,3,2,1,0:T(8,128)(2,1)}, bf16[2,2,16,32,1536]{4,3,2,1,0:T(8,128)(2,1)}) custom-call(s32[4]{0:T(128)S(1)} %copy-done.3, s32[4]{0:T(128)S(1)} %copy-done.2, bf16[2,51,2,4,32,512]{5,4,3,2,1,0:T(8,128)(2,1)} %get-tuple-element.10.hist, ...), custom_call_target="tpu_custom_call" | custom-call | tf_op jit(solution)/shard_map/place_slots/pallas_call | solution.py:482
  318.3 0.0 copy-done.4
  318.3 0.7 copy.45
  (6 shorter events, 0.0 us)
Async XLA Ops:
  301.1 2.8 copy-start
  303.9 2.8 copy-start.1
  306.7 0.7 copy-start.2
  307.3 0.7 copy-start.3
  308.0 10.3 %copy-start.4 = (bf16[64,1536]{1,0:T(8,128)(2,1)S(1)}, bf16[64,1536]{1,0:T(8,128)(2,1)}, u32[]{:S(2)}) copy-start(bf16[64,1536]{1,0:T(8,128)(2,1)} %get-tuple-element.30) | copy-start | bytes 589828

commit v3 on v2

--- a/solution.py
+++ b/solution.py
@@ -29,12 +29,18 @@
     return jnp.concatenate(cols, axis=1)
 
 
-SUB = 32
 CELLS = 4
+SUM_PARTS = 4
+MOVE_PARTS = 4
+TOK_PARTS = 2
+
+
+def piece_rows(ff):
+    return max(ff // 8, 32)
 
 
 def unit_counts(dim, ff):
-    per_block, blocks = ff // 4 // SUB, dim // ff
+    per_block, blocks = ff // 4 // piece_rows(ff), dim // ff
     return per_block, blocks, 3 * blocks * per_block
 
 
@@ -76,8 +82,11 @@
 
     mine, theirs = pl.ds(0, rows), pl.ds(rows, rows)
 
-    def xcopy(l, s, d):
-        return remote(xb.at[l, s, part(d)], xb.at[l, s + 1, part(d)], xsend.at[l, s, d], xrecv.at[l, s + 1, d], peers[d])
+    bit = half // TOK_PARTS
+
+    def xcopy(l, s, d, p):
+        r = pl.ds(d * half + p * bit, bit)
+        return remote(xb.at[l, s, r], xb.at[l, s + 1, r], xsend.at[l, s, d, p], xrecv.at[l, s + 1, d, p], peers[d])
 
     def mcopy(l, s):
         return remote(xb.at[l, s, mine], xb.at[l, s, theirs], msend.at[l, s], mrecv.at[l, s], mate)
@@ -91,18 +100,28 @@
     def pcopy(l, s):
         return remote(pcs.at[lax.rem(s, 2)], pcr.at[s], psend.at[lax.rem(s, 2)], precv.at[l, s], mate)
 
-    def rcopy(l, s, d):
-        return remote(rs.at[s, part(d)], rs.at[s + 1, part(d)], rsend.at[l, s, d], rrecv.at[l, s + 1, d], peers[d])
+    strip = half // SUM_PARTS
+
+    def strips(p):
+        return [pl.ds(d * half + p * strip, strip) for d in range(2)]
+
+    def rcopy(l, s, d, p):
+        rows_p = strips(p)[d]
+        return remote(rs.at[s, rows_p], rs.at[s + 1, rows_p], rsend.at[l, s, d, p], rrecv.at[l, s + 1, d, p], peers[d])
 
     per_block, blocks, units = unit_counts(dim, ff)
+    SUB = piece_rows(ff)
     per_matrix = blocks * per_block
     total_moves = src.shape[0]
     per_layer = total_moves // layers
     trips = units + n - 1
     quarter = ff // 4
 
-    def ocopy(t, d):
-        return remote(obuf.at[lax.rem(t, 2), d], cell.at[lax.rem(t, CELLS), d], osend.at[lax.rem(t, 2), d], orecv.at[lax.rem(t, CELLS), d], peers[d])
+    some = total_moves // MOVE_PARTS
+
+    def ocopy(t, d, h):
+        o, c, ms = lax.rem(t, 2), lax.rem(t, CELLS), pl.ds(h * some, some)
+        return remote(obuf.at[o, d, ms], cell.at[c, d, ms], osend.at[o, d, h], orecv.at[c, d, h], peers[d])
 
     def hcopy(t):
         return remote(cell.at[lax.rem(t, CELLS)], hist.at[1, t], hsend.at[lax.rem(t, 2)], hrecv.at[t], mate)
@@ -149,7 +168,7 @@
         by_matrix(t, fill)
         vcopy(t).start()
 
-    def convey(t):
+    def convey(t, between=None):
         last = lax.rem(t + CELLS - 1, CELLS)
         slot = lax.rem(t, 2)
 
@@ -163,13 +182,6 @@
             for d in range(2):
                 pl.semaphore_signal(cred.at[d], inc=1, device_id={'ep': peers[1 - d]}, device_id_type=MESH)
 
-        @pl.when((t >= 1) & (t <= trips))
-        def _():
-            for d in range(2):
-                ocopy(t - 1, d).wait_recv()
-            hkeep(t - 1).start()
-            hcopy(t - 1).start()
-
         @pl.when(t < trips)
         def _():
             @pl.when(t >= CELLS - 1)
@@ -180,35 +192,54 @@
             @pl.when(t >= 2)
             def _():
                 for d in range(2):
-                    ocopy(t - 2, d).wait_send()
+                    for h in range(MOVE_PARTS):
+                        ocopy(t - 2, d, h).wait_send()
 
             @pl.when(t < units)
             def _():
                 vcopy(t).wait_recv()
 
-                def fill(m):
-                    for d in range(2):
-                        for mv in range(total_moves):
-                            holder = lax.div(src[mv], slots)
-                            val = jnp.where(holder == mate, cin[slot, d, mv], cell[last, d, mv])
-                            obuf[slot, d, mv] = jnp.where(holder == me, own_piece(m, t, mv, 2 * core + d), val)
-
-                by_matrix(t, fill)
-
-                @pl.when(t < units - 2)
-                def _():
-                    pl.semaphore_signal(vcred, inc=1, device_id={'ep': mate}, device_id_type=MESH)
-
-            @pl.when(t >= units)
-            def _():
-                obuf[slot] = cell[last]
-
-            for d in range(2):
-                ocopy(t, d).start()
-
-            @pl.when(t + 1 < units)
-            def _():
-                offer(t + 1)
+        for h in range(MOVE_PARTS):
+            @pl.when((t >= 1) & (t <= trips))
+            def _():
+                for d in range(2):
+                    ocopy(t - 1, d, h).wait_recv()
+
+            def fill(m):
+                for d in range(2):
+                    for mv in range(h * some, (h + 1) * some):
+                        holder = lax.div(src[mv], slots)
+                        val = jnp.where(holder == mate, cin[slot, d, mv], cell[last, d, mv])
+                        obuf[slot, d, mv] = jnp.where(holder == me, own_piece(m, t, mv, 2 * core + d), val)
+
+            by_matrix(t, fill)
+
+            @pl.when((t >= units) & (t < trips))
+            def _():
+                for d in range(2):
+                    for mv in range(h * some, (h + 1) * some):
+                        obuf[slot, d, mv] = cell[last, d, mv]
+
+            @pl.when(t < trips)
+            def _():
+                for d in range(2):
+                    ocopy(t, d, h).start()
+
+            if between is not None:
+                between(h)
+
+        @pl.when((t >= 1) & (t <= trips))
+        def _():
+            hkeep(t - 1).start()
+            hcopy(t - 1).start()
+
+        @pl.when(t < units - 2)
+        def _():
+            pl.semaphore_signal(vcred, inc=1, device_id={'ep': mate}, device_id_type=MESH)
+
+        @pl.when(t + 1 < units)
+        def _():
+            offer(t + 1)
 
     def shared_loads(l):
         return [pltpu.make_async_copy(src.at[l], dst, ssem.at[l, i]) for i, (src, dst) in enumerate(((sg, sgv), (su, suv), (sd, sdv)))]
@@ -235,10 +266,10 @@
     tok_in.wait()
     coef_in.wait()
 
-    def forward(l, s):
+    def forward(l, s, p):
         for d in range(2):
-            xcopy(l, s, d).start()
-            if l == 0:
+            xcopy(l, s, d, p).start()
+            if l == 0 and p == TOK_PARTS - 1:
                 ccopy(s, d).start()
 
     def to_mate(l, s):
@@ -246,10 +277,10 @@
         if l == 0:
             cmcopy(s).start()
 
-    def wait_block(l, s):
+    def wait_block(l, s, p):
         for d in range(2):
-            xcopy(l, s - 1, d).wait_recv()
-            if l == 0:
+            xcopy(l, s - 1, d, p).wait_recv()
+            if l == 0 and p == TOK_PARTS - 1:
                 ccopy(s - 1, d).wait_recv()
 
     def wait_mate(l, s):
@@ -282,7 +313,8 @@
             pcs[slot, :, c:c + dblk] = total[rows:]
 
     for l in range(layers):
-        forward(l, 0)
+        for p in range(TOK_PARTS):
+            forward(l, 0, p)
         to_mate(l, 0)
         if l > 0:
             drain(l - 1)
@@ -313,18 +345,50 @@
             offer(0)
         if l > 0:
             pl.semaphore_wait(mid, 3)
+        first_trip = l * (n + 2)
+        convey(jnp.int32(first_trip))
         wait_mate(l, 0)
         experts(l, 0)
         pcopy(l, 0).start()
         hacc[...] += own[...]
-        wait_block(l, 1)
-        forward(l, 1)
+        for p in range(TOK_PARTS):
+            wait_block(l, 1, p)
+            forward(l, 1, p)
         to_mate(l, 1)
+        convey(jnp.int32(first_trip + 1))
 
         def step(s, carry):
-            trip = 2 * (l * (n - 1) + s - 1)
-            convey(trip)
+            def come(p):
+                @pl.when(s < n - 1)
+                def _():
+                    wait_block(l, s + 1, p)
+
+                @pl.when(s < n - 2)
+                def _():
+                    forward(l, s + 1, p)
+
+            def send_sums(h):
+                if h == 0:
+                    pcopy(l, s).wait_recv()
+                for p in range(h * SUM_PARTS // MOVE_PARTS, (h + 1) * SUM_PARTS // MOVE_PARTS):
+                    @pl.when(s == 1)
+                    def _():
+                        for r in strips(p):
+                            rs[s, r] = own[r] + pcr[s, r]
+
+                    @pl.when(s > 1)
+                    def _():
+                        for d in range(2):
+                            rcopy(l, s - 1, d, p).wait_recv()
+                        for r in strips(p):
+                            rs[s, r] = rs[s, r] + (own[r] + pcr[s, r])
+
+                    for d in range(2):
+                        rcopy(l, s, d, p).start()
+
             wait_mate(l, s)
+            for p in range(TOK_PARTS - 1):
+                come(p)
 
             @pl.when(s >= 2)
             def _():
@@ -332,36 +396,20 @@
 
             experts(l, s)
             pcopy(l, s).start()
+            come(TOK_PARTS - 1)
 
             @pl.when(s < n - 1)
             def _():
-                wait_block(l, s + 1)
                 to_mate(l, s + 1)
 
-            @pl.when(s < n - 2)
-            def _():
-                forward(l, s + 1)
-
-            convey(trip + 1)
-            pcopy(l, s).wait_recv()
-
-            @pl.when(s == 1)
-            def _():
-                rs[s] = own[...] + pcr[s]
-
-            @pl.when(s > 1)
-            def _():
-                for d in range(2):
-                    rcopy(l, s - 1, d).wait_recv()
-                rs[s] = rs[s] + (own[...] + pcr[s])
-
-            for d in range(2):
-                rcopy(l, s, d).start()
+            convey(first_trip + s + 1, send_sums)
             return carry
 
         lax.fori_loop(1, n, step, 0)
+        convey(jnp.int32(first_trip + n + 1))
         for d in range(2):
-            rcopy(l, n - 1, d).wait_recv()
+            for p in range(SUM_PARTS):
+                rcopy(l, n - 1, d, p).wait_recv()
         pcopy(l, 0).wait_recv()
         new_h = (hacc[...] + (pcr[0] + rs[n])).astype(BF16)
         if l + 1 < layers:
@@ -376,7 +424,8 @@
             if l == 0:
                 cmcopy(0).wait_send()
             for d in range(2):
-                xcopy(l, 0, d).wait_send()
+                for p in range(TOK_PARTS):
+                    xcopy(l, 0, d, p).wait_send()
                 if l == 0:
                     ccopy(0, d).wait_send()
 
@@ -385,12 +434,14 @@
                 if l == 0:
                     cmcopy(s).wait_send()
                 for d in range(2):
-                    rcopy(l, s, d).wait_send()
+                    for p in range(SUM_PARTS):
+                        rcopy(l, s, d, p).wait_send()
 
                 @pl.when(s < n - 1)
                 def _():
                     for d in range(2):
-                        xcopy(l, s, d).wait_send()
+                        for p in range(TOK_PARTS):
+                            xcopy(l, s, d, p).wait_send()
                         if l == 0:
                             ccopy(s, d).wait_send()
                 return carry
@@ -400,7 +451,8 @@
     drain(layers - 1)
     for t in (trips - 2, trips - 1):
         for d in range(2):
-            ocopy(t, d).wait_send()
+            for h in range(MOVE_PARTS):
+                ocopy(t, d, h).wait_send()
     for t in (units - 2, units - 1):
         vcopy(t).wait_send()
 
@@ -416,7 +468,7 @@
     n = side * side
     per_layer = src.shape[0] // layers
     ff = hist.shape[-1]
-    per_block = ff // 4 // SUB
+    per_block = ff // 4 // piece_rows(ff)
     blocks = wg.shape[2] // (4 * per_block)
     me = lax.axis_index('ep')
 
@@ -476,6 +528,7 @@
 
 def place_weights(src, slot_to, hist, weights, side):
     layers, slots = weights[0].shape[:2]
+    SUB = piece_rows(weights[0].shape[3])
     split = [w.reshape(layers, slots, w.shape[2] // SUB, SUB, w.shape[3]) for w in weights]
     any_spec = pl.BlockSpec(memory_space=pl.ANY)
     smem = pl.BlockSpec(memory_space=pltpu.SMEM)
@@ -485,7 +538,7 @@
         in_specs=[smem, smem] + [any_spec] * 4,
         out_specs=[any_spec] * 3,
         scratch_shapes=[pltpu.VMEM(w.shape, w.dtype) for w in split] + [pltpu.SemaphoreType.DMA((layers, slots, 3))] * 2,
-        compiler_params=pltpu.CompilerParams(vmem_limit_bytes=40 << 20),
+        compiler_params=pltpu.CompilerParams(vmem_limit_bytes=67043328),
         name='place_slots',
     )(src, slot_to, hist, *split)
     return tuple(o.reshape(w.shape) for o, w in zip(out, weights))
@@ -505,8 +558,8 @@
     per_block, blocks, units = unit_counts(dim, ff)
     trips = units + n - 1
     moves = src.shape[0]
-    assert 2 * layers * (n - 1) > trips + 1 and units > 2
-    piece = (2, moves, SUB, ff)
+    assert layers * (n + 3) - 1 > trips + 1 and units > 2
+    piece = (2, moves, piece_rows(ff), ff)
     scratch = [
         vmem((CELLS,) + piece, BF16),
         vmem((2,) + piece, BF16),
@@ -527,13 +580,13 @@
         vmem((n, rows, dim), F32),
         vmem((n + 1, rows, dim), F32),
         dma((layers, 3)), dma((layers, 3)), dma((2,)),
-        dma((layers, n, 2)), dma((layers, n, 2)),
+        dma((layers, n, 2, TOK_PARTS)), dma((layers, n, 2, TOK_PARTS)),
         dma((layers, n)), dma((layers, n)),
         dma((n, 2)), dma((n, 2)),
         dma((n,)), dma((n,)),
         dma((2,)), dma((layers, n)),
-        dma((layers, n, 2)), dma((layers, n + 1, 2)),
-        dma((2, 2)), dma((CELLS, 2)), dma((2,)), dma((2,)), dma((trips,)), dma((2,)), dma((2,)),
+        dma((layers, n, 2, SUM_PARTS)), dma((layers, n + 1, 2, SUM_PARTS)),
+        dma((2, 2, MOVE_PARTS)), dma((CELLS, 2, MOVE_PARTS)), dma((2,)), dma((2,)), dma((trips,)), dma((2,)), dma((2,)),
         pltpu.SemaphoreType.REGULAR((2,)), pltpu.SemaphoreType.REGULAR,
         pltpu.SemaphoreType.REGULAR,
     ]

time: 319 us -> 249 us (0.78)
  Pallas kernels: 304 us -> 239 us
  local copies, waits for them, and re-layouts: 11.9 us -> 5.99 us
    pallas_call x1, Pallas kernels: 294 us -> 225 us  [moe(): pl.pallas_call(functools.partial(moe_kernel, side), out_shape=[jax.ShapeD...]
    unnamed x15 -> x5, local copies, waits for them, and re-layouts: 7.58 us -> 1.63 us
    pallas_call x1, Pallas kernels: 10.3 us -> 14.1 us  [place_weights(): pl.pallas_call(functools.partial(place_kernel, side), out_shape=[jax.Shap...]
where the time goes in v3:
time: 249 us; the launch traced here: 248 us
  Pallas kernels  239 us (96%)
  local copies, waits for them, and re-layouts  5.99 us (2%)
    pallas_call x1, Pallas kernels, moe(): pl.pallas_call(functools.partial(moe_kernel, side), out_shape=[jax.ShapeD...  225 us
    pallas_call x1, Pallas kernels, place_weights(): pl.pallas_call(functools.partial(place_kernel, side), out_shape=[jax.Shap...  14.1 us

profile of v3, /device:TPU:98, one launch (start us, length us, event | category | flops | bytes accessed | tf_op | source)
XLA Modules:
  0.0 247.8 jit_solution(8960977071126376736)
XLA Ops:
  0.6 1.3 reshape.51.slot_to
  1.9 0.8 slice_bitcast_fusion.3
  2.7 0.2 select_reduce_fusion.3
  2.9 0.2 select_reduce_fusion.2
  3.1 0.8 slice_bitcast_fusion.2
  3.8 0.2 fusion
  4.0 0.6 pad_add_fusion.src
  4.6 0.8 fusion.2
  5.4 0.8 fusion.3
  6.2 0.3 select_reduce_fusion
  6.5 0.7 pad_maximum_fusion.coef
  7.2 224.9 %moe_rings.1 = (bf16[64,1536]{1,0:T(8,128)(2,1)}, bf16[2,33,2,4,64,512]{5,4,3,2,1,0:T(8,128)(2,1)}) custom-call(s32[4]{0:T(128)} %pad_add_fusion.src, bf16[64,1536]{1,0:T(8,128)(2,1)} %tok.1, f32[64,128]{1,0:T(8,128)} %pad_maximum_fusion.coef, bf16[2,2,1536,512]{3,2,1,0:T(8,128)(2,1)} %wg.1, bf16[2,2,1536,512]{3,2,1,0:T(8,128)(2,1)} %wu.1, ...), custom_call_target="tpu_custom_call" | custom-call | flops 159450660864 | bytes 41943040 | tf_op jit(solution)/shard_map/moe_rings/pallas_call | solution.py:594
  232.1 14.1 %place_slots.1 = (bf16[2,2,24,64,512]{4,3,2,1,0:T(8,128)(2,1)}, bf16[2,2,24,64,512]{4,3,2,1,0:T(8,128)(2,1)}, bf16[2,2,8,64,1536]{4,3,2,1,0:T(8,128)(2,1)}) custom-call(s32[4]{0:T(128)} %pad_add_fusion.src, s32[4]{0:T(128)} %reshape.51.slot_to, bf16[2,33,2,4,64,512]{5,4,3,2,1,0:T(8,128)(2,1)} %get-tuple-element.10.hist, ...), custom_call_target="tpu_custom_call" | custom-call | tf_op jit(solution)/shard_map/place_slots/pallas_call | solution.py:535
  246.2 1.6 copy.45
  (6 shorter events, 0.0 us)
